TPU v7x, 16 devices: a whole 2x2x2 slice. The times are simulated.
16 devices in a mesh: dp: 2 (over z), cp: 8 (over y, x, core).
Axes of the slice: x: 2, y: 2, z: 2, core: 2. Of those that a mesh axis runs over, the one named last changes fastest.
Arguments:
- latent: bfloat16 [32, 6, 96, 512], P(('dp', 'cp')), parts along dimension 0
- conv_kernels: bfloat16 [4, 3, 3, 3, 512, 512], replicated
- conv_biases: float32 [4, 512], replicated
- gn_gammas: float32 [4, 512], replicated
- gn_betas: float32 [4, 512], replicated
Outputs:
- output: bfloat16 [32, 6, 96, 512], P(('dp', 'cp')), parts along dimension 0
There are 2 independent parts. A program takes and returns all parts, laid end to end along the dimension named above; an argument that names none is the same for every part.
All inputs are finite; a program needn't handle non-finite values.
Results may differ from a plain program's by a relative error of at most 0.0125181.
Values are sent between devices in bfloat16 or wider.
A program may use at most 1 GiB of HBM per device.

v0:
```python
import jax
import jax.numpy as jnp
from jax import lax
from jax.sharding import PartitionSpec as P

GROUPS = 32
NORM_EPS = 1e-6


def group_sums(hidden):
    n_frames, n_rows, n_cols, n_chans = hidden.shape
    grouped = hidden.astype(jnp.float32).reshape(n_frames, n_rows, n_cols, GROUPS, n_chans // GROUPS)
    return jnp.stack([jnp.sum(grouped, axis=(0, 1, 2, 4)), jnp.sum(grouped * grouped, axis=(0, 1, 2, 4))])


def norm_act(hidden, grp_sums, elem_count, gn_gamma, gn_beta):
    grp_mean = grp_sums[0] / elem_count
    grp_var = grp_sums[1] / elem_count - grp_mean * grp_mean
    group_width = hidden.shape[-1] // GROUPS
    chan_scale = jnp.repeat(lax.rsqrt(grp_var + NORM_EPS), group_width) * gn_gamma
    chan_shift = gn_beta - jnp.repeat(grp_mean, group_width) * chan_scale
    normed = (hidden.astype(jnp.float32) * chan_scale + chan_shift).astype(jnp.bfloat16)
    return jax.nn.silu(normed.astype(jnp.float32)).astype(jnp.bfloat16)


def conv_frames(padded, kernel, conv_bias):
    result = lax.conv_general_dilated(padded[None], kernel, window_strides=(1, 1, 1), padding=((0, 0), (1, 1), (1, 1)), dimension_numbers=("NDHWC", "DHWIO", "NDHWC"), preferred_element_type=jnp.float32)[0]
    return (result + conv_bias).astype(jnp.bfloat16)


def solution(mesh):
    n_time = mesh.shape["cp"]
    next_perm = [(src, src + 1) for src in range(n_time - 1)]
    frame_spec = P(("dp", "cp"))

    def local_fn(latent, conv_kernels, conv_biases, gn_gammas, gn_betas):
        n_frames, n_rows, n_cols, n_chans = latent.shape
        my_rank = lax.axis_index("cp")
        elem_count = n_time * n_frames * n_rows * n_cols * (n_chans // GROUPS)

        def gn_step(hidden, layer_idx):
            grp_sums = lax.psum(group_sums(hidden), "cp")
            return norm_act(hidden, grp_sums, elem_count, gn_gammas[layer_idx], gn_betas[layer_idx])

        def conv_step(act_in, layer_idx):
            from_prev = lax.ppermute(act_in[n_frames - 2:], "cp", next_perm)
            own_first = jnp.concatenate([act_in[:1], act_in[:1]], axis=0)
            halo_frames = jnp.where(my_rank == 0, own_first, from_prev)
            return conv_frames(jnp.concatenate([halo_frames, act_in], axis=0), conv_kernels[layer_idx], conv_biases[layer_idx])

        hidden = latent
        for block_idx in range(2):
            first_layer = 2 * block_idx
            inner = conv_step(gn_step(hidden, first_layer), first_layer)
            inner = conv_step(gn_step(inner, first_layer + 1), first_layer + 1)
            hidden = (hidden.astype(jnp.float32) + inner.astype(jnp.float32)).astype(jnp.bfloat16)
        return hidden

    return jax.shard_map(local_fn, mesh=mesh, in_specs=(frame_spec, P(), P(), P(), P()), out_specs=frame_spec, check_vma=False)
```

profile of v0, /device:TPU:12, one launch (start us, length us, event | category | flops | bytes accessed | tf_op | source)
XLA Modules:
  0.0 263.5 jit_solution(8398827353631729136)
XLA Ops:
  0.0 1.7 convert_reduce_fusion.1
  2.1 12.7 %psum.28 = f32[2,32]{1,0:T(2,128)S(1)} all-reduce(f32[2,32]{1,0:T(2,128)S(1)} %pad_maximum_fusion), channel_id=1, replica_groups=mesh['dp'=2,'cp'=8] {'cp'}, use_global_device_ids=true, to_apply=%region_4.5 | all-reduce | flops 64 | bytes 512 | tf_op jit(solution)/shard_map/psum | solution.py:42
  14.7 0.9 fusion.124
  16.8 1.9 fusion.49
  18.7 1.9 collective-permute-start
  21.3 15.8 %collective-permute-done = bf16[2,6,96,512]{3,2,1,0:T(8,128)(2,1)S(1)} collective-permute-done((bf16[2,6,96,512]{3,2,1,0:T(8,128)(2,1)S(1)}, bf16[2,6,96,512]{3,2,1,0:T(8,128)(2,1)S(1)}, u32[]{:S(2)}, u32[]{:S(2)}) %collective-permute-start) | collective-permute-done | bytes 1179680 | tf_op jit(solution)/shard_map/ppermute | solution.py:46
  37.5 1.8 copy.44
  39.3 1.0 pad.clone
  41.0 25.2 %fusion.40 = (f32[512]{0:T(512)S(1)}, f32[512]{0:T(512)S(1)}, f32[2,6,8,13,512]{4,2,3,1,0:T(8,128)S(1)}) fusion(pred[8,13]{0,1:T(8,128)(4,1)S(1)} %copy-done.3, f32[512]{0:T(512)S(1)} %bitcast.169, bf16[4,3,3,3,512,512]{5,4,3,2,1,0:T(8,128)(2,1)} %param.6, bf16[4,6,1,7,2,512]{5,3,4,1,0,2:T(8,128)(2,1)S(1)} %slice.125, ...), kind=kOutput, calls=%fused_computation.57 | convolution fusion | flops 15718072320 | bytes 19617896 | tf_op jit(solution)/shard_map/conv_general_dilated | solution.py:27
  66.6 12.0 %psum.29 = f32[2,32]{1,0:T(2,128)S(1)} all-reduce(f32[2,32]{1,0:T(2,128)S(1)} %pad_maximum_fusion.1), channel_id=1, replica_groups=mesh['dp'=2,'cp'=8] {'cp'}, use_global_device_ids=true, to_apply=%region_9.10 | all-reduce | flops 64 | bytes 512 | tf_op jit(solution)/shard_map/psum | solution.py:42
  78.9 2.0 copy.23
  82.5 1.9 collective-permute-start.1
  84.4 16.4 %collective-permute-done.1 = bf16[2,6,96,512]{3,2,1,0:T(8,128)(2,1)S(1)} collective-permute-done((bf16[2,6,96,512]{3,2,1,0:T(8,128)(2,1)S(1)}, bf16[2,6,96,512]{3,2,1,0:T(8,128)(2,1)S(1)}, u32[]{:S(2)}, u32[]{:S(2)}) %collective-permute-start.1) | collective-permute-done | bytes 1179680 | tf_op jit(solution)/shard_map/ppermute | solution.py:46
  101.3 1.8 copy.45
  103.1 1.0 pad.2.clone
  104.7 25.5 %fusion.87 = f32[2,6,8,13,512]{4,2,3,1,0:T(8,128)S(1)} fusion(bf16[4,3,3,3,512,512]{5,4,3,2,1,0:T(8,128)(2,1)} %param.6, bf16[4,6,1,7,2,512]{5,3,4,1,0,2:T(8,128)(2,1)S(1)} %slice.128, bf16[4,6,1,8,13,512]{5,3,4,1,0,2:T(8,128)(2,1)S(1)} %copy.27, pred[8,13]{0,1:T(8,128)(4,1)S(1)} %copy-done.3), kind=kOutput, calls=%fused_computation.112 | convolution fusion | flops 15712960512 | bytes 19611752 | tf_op jit(solution)/shard_map/conv_general_dilated | solution.py:27
  130.1 2.0 copy.28
  134.4 11.8 %psum.30 = f32[2,32]{1,0:T(2,128)S(1)} all-reduce(f32[2,32]{1,0:T(2,128)S(1)} %pad_maximum_fusion.2), channel_id=1, replica_groups=mesh['dp'=2,'cp'=8] {'cp'}, use_global_device_ids=true, to_apply=%region_14.15 | all-reduce | flops 64 | bytes 512 | tf_op jit(solution)/shard_map/psum | solution.py:42
  147.3 1.9 collective-permute-start.2
  149.2 16.4 %collective-permute-done.2 = bf16[2,6,96,512]{3,2,1,0:T(8,128)(2,1)S(1)} collective-permute-done((bf16[2,6,96,512]{3,2,1,0:T(8,128)(2,1)S(1)}, bf16[2,6,96,512]{3,2,1,0:T(8,128)(2,1)S(1)}, u32[]{:S(2)}, u32[]{:S(2)}) %collective-permute-start.2) | collective-permute-done | bytes 1179680 | tf_op jit(solution)/shard_map/ppermute | solution.py:46
  166.0 1.8 copy.46
  167.9 1.0 pad.4.clone
  169.5 23.5 %fusion.43 = (f32[512]{0:T(512)S(1)}, f32[512]{0:T(512)S(1)}, f32[2,6,8,13,512]{4,2,3,1,0:T(8,128)}) fusion(pred[8,13]{0,1:T(8,128)(4,1)S(1)} %copy-done.3, f32[512]{0:T(512)S(1)} %bitcast.167, bf16[4,3,3,3,512,512]{5,4,3,2,1,0:T(8,128)(2,1)} %param.6, bf16[4,6,1,7,2,512]{5,3,4,1,0,2:T(8,128)(2,1)S(1)} %slice.131, bf16[4,6,1,8,13,512]{5,3,4,1,0,2:T(8,128)(2,1)S(1)} %copy.32), kind=kOutput, calls=%fused_computation.60 | convolution fusion | flops 15718072320 | bytes 19617896 | tf_op jit(solution)/shard_map/conv_general_dilated | solution.py:27
  193.3 12.0 %psum.31 = f32[2,32]{1,0:T(2,128)S(1)} all-reduce(f32[2,32]{1,0:T(2,128)S(1)} %pad_maximum_fusion.3), channel_id=1, replica_groups=mesh['dp'=2,'cp'=8] {'cp'}, use_global_device_ids=true, to_apply=%region_19.20 | all-reduce | flops 64 | bytes 512 | tf_op jit(solution)/shard_map/psum | solution.py:42
  205.7 3.7 %copy.33 = f32[2,6,8,13,512]{4,0,3,2,1:T(2,128)S(1)} copy(f32[2,6,8,13,512]{4,2,3,1,0:T(8,128)} %get-tuple-element.35) | data formatting | bytes 5111808 | tf_op jit(solution)/shard_map/conv_general_dilated | solution.py:27
  211.0 1.9 collective-permute-start.3
  213.0 16.4 %collective-permute-done.3 = bf16[2,6,96,512]{3,2,1,0:T(8,128)(2,1)S(1)} collective-permute-done((bf16[2,6,96,512]{3,2,1,0:T(8,128)(2,1)S(1)}, bf16[2,6,96,512]{3,2,1,0:T(8,128)(2,1)S(1)}, u32[]{:S(2)}, u32[]{:S(2)}) %collective-permute-start.3) | collective-permute-done | bytes 1179680 | tf_op jit(solution)/shard_map/ppermute | solution.py:46
  229.8 1.8 copy.47
  231.6 1.0 pad.6.clone
  233.2 25.4 %fusion.97 = f32[2,6,8,13,512]{4,2,3,1,0:T(8,128)S(1)} fusion(bf16[4,3,3,3,512,512]{5,4,3,2,1,0:T(8,128)(2,1)} %param.6, bf16[4,6,1,7,2,512]{5,3,4,1,0,2:T(8,128)(2,1)S(1)} %slice.134, bf16[4,6,1,8,13,512]{5,3,4,1,0,2:T(8,128)(2,1)S(1)} %copy.37, pred[8,13]{0,1:T(8,128)(4,1)S(1)} %copy-done.3), kind=kOutput, calls=%fused_computation.114 | convolution fusion | flops 15712960512 | bytes 19611752 | tf_op jit(solution)/shard_map/conv_general_dilated | solution.py:27
  258.6 2.0 copy.38
  261.4 1.5 fusion.69
  (86 shorter events, 14.9 us)
Async XLA Ops:
  0.0 20.7 %copy-start.2 = (f32[4,512]{1,0:T(4,128)S(1)}, f32[4,512]{1,0:T(4,128)}, u32[]{:S(2)}) copy-start(f32[4,512]{1,0:T(4,128)} %param.7) | copy-start | bytes 24580
  18.7 18.4 %collective-permute-start = (bf16[2,6,96,512]{3,2,1,0:T(8,128)(2,1)S(1)}, bf16[2,6,96,512]{3,2,1,0:T(8,128)(2,1)S(1)}, u32[]{:S(2)}, u32[]{:S(2)}) collective-permute-start(bf16[2,6,96,512]{3,2,1,0:T(8,128)(2,1)S(1)} %fusion.49), channel_id=1, source_target_pairs={{0,1},{1,2},{2,3},{3,4},{4,5},{5,6},{6,7},{8,9},{9,10},{10,11},{11... | collective-permute-start | bytes 3538952 | tf_op jit(solution)/shard_map/ppermute | solution.py:46
  40.3 0.7 copy-start.3
  82.5 18.4 %collective-permute-start.1 = (bf16[2,6,96,512]{3,2,1,0:T(8,128)(2,1)S(1)}, bf16[2,6,96,512]{3,2,1,0:T(8,128)(2,1)S(1)}, u32[]{:S(2)}, u32[]{:S(2)}) collective-permute-start(bf16[2,6,96,512]{3,2,1,0:T(8,128)(2,1)S(1)} %fusion.53), channel_id=1, source_target_pairs={{0,1},{1,2},{2,3},{3,4},{4,5},{5,6},{6,7},{8,9},{9,10},{10,11},{11... | collective-permute-start | bytes 3538952 | tf_op jit(solution)/shard_map/ppermute | solution.py:46
  132.1 1.3 copy-start
  147.3 18.4 %collective-permute-start.2 = (bf16[2,6,96,512]{3,2,1,0:T(8,128)(2,1)S(1)}, bf16[2,6,96,512]{3,2,1,0:T(8,128)(2,1)S(1)}, u32[]{:S(2)}, u32[]{:S(2)}) collective-permute-start(bf16[2,6,96,512]{3,2,1,0:T(8,128)(2,1)S(1)} %fusion.57), channel_id=1, source_target_pairs={{0,1},{1,2},{2,3},{3,4},{4,5},{5,6},{6,7},{8,9},{9,10},{10,11},{11... | collective-permute-start | bytes 3538952 | tf_op jit(solution)/shard_map/ppermute | solution.py:46
  211.0 18.4 %collective-permute-start.3 = (bf16[2,6,96,512]{3,2,1,0:T(8,128)(2,1)S(1)}, bf16[2,6,96,512]{3,2,1,0:T(8,128)(2,1)S(1)}, u32[]{:S(2)}, u32[]{:S(2)}) collective-permute-start(bf16[2,6,96,512]{3,2,1,0:T(8,128)(2,1)S(1)} %fusion.61), channel_id=1, source_target_pairs={{0,1},{1,2},{2,3},{3,4},{4,5},{5,6},{6,7},{8,9},{9,10},{10,11},{11... | collective-permute-start | bytes 3538952 | tf_op jit(solution)/shard_map/ppermute | solution.py:46
  260.6 0.8 copy-start.1
where the time goes:
time: 268 us; the launch traced here: 263 us
  matrix products  99.5 us (37%)
  waiting for transfers between devices  65.1 us (24%)
  blocking collectives  48.5 us (18%)
  local copies, waits for them, and re-layouts  31.3 us (12%)
  other arithmetic  10.4 us (4%)
  starting transfers between devices  7.68 us (3%)
    conv_general_dilated x4, matrix products, conv_frames(): lax.conv_general_dilated(padded[None], kernel, window_strides=(1, 1, 1),...  99.5 us
    ppermute x4, waiting for transfers between devices, conv_step(): from_prev = lax.ppermute(act_in[n_frames - 2:], 'cp', next_perm)  65.1 us
    psum x4, blocking collectives, gn_step(): grp_sums = lax.psum(group_sums(hidden), 'cp')  48.5 us
    conv_general_dilated x16, local copies, waits for them, and re-layouts, conv_frames(): lax.conv_general_dilated(padded[None], kernel, window_strides=(1, 1, 1),...  15.3 us
    unnamed x12, local copies, waits for them, and re-layouts  7.82 us
    ppermute x4, starting transfers between devices, conv_step(): from_prev = lax.ppermute(act_in[n_frames - 2:], 'cp', next_perm)  7.68 us
  transfers between devices with their start and end apart: 4, of which 4 were waited for; matrix products, arithmetic and copies ran while one was open for 0% of the time, Pallas kernels for 0%

commit v1 on v0

v1 whole, which is shorter than its diff:
```python
import jax
import jax.numpy as jnp
from jax import lax
from jax.experimental import pallas as pl
from jax.experimental.pallas import tpu as pltpu
from jax.sharding import PartitionSpec as P

MESH = pl.DeviceIdType.MESH
F32, BF16 = jnp.float32, jnp.bfloat16
GROUPS = 32
NORM_EPS = 1e-6
N_LAYERS = 4
ROWS = 6
WIDTH = 96
LANES = 16
RES = 6
CHANS = 512
TILE = 256


def kernel(n_time, lat_ref, w_ref, bias_ref, gam_ref, bet_ref, out_ref,
           raw, xbuf, acc0, acc1, a0, a1, a2, a3, wbuf, affine, pstat, srecv,
           lat_sem, w_sem, stat_send, stat_recv, halo_send, halo_recv, out_sem):
    me = lax.axis_index("cp")
    nxt = lax.rem(me + 1, n_time)
    acts = (a0, a1, a2, a3)

    barrier = pltpu.get_barrier_semaphore()
    for d in range(1, n_time):
        pl.semaphore_signal(barrier, inc=1, device_id={"cp": lax.rem(me + d, n_time)}, device_id_type=MESH)

    def weights_copy(layer, k):
        slot = lax.rem(layer, 2)
        return pltpu.make_async_copy(w_ref.at[layer, k], wbuf.at[slot, k], w_sem.at[slot, k])

    def halo_copy(frame, par):
        return pltpu.make_async_remote_copy(
            src_ref=raw.at[frame], dst_ref=raw.at[2 + 2 * par + frame],
            send_sem=halo_send.at[frame], recv_sem=halo_recv.at[par, frame],
            device_id={"cp": nxt}, device_id_type=MESH)

    lat_copy = pltpu.make_async_copy(lat_ref, raw.at[pl.ds(0, 2)], lat_sem.at[0])
    x_copy = pltpu.make_async_copy(lat_ref, xbuf, lat_sem.at[1])
    lat_copy.start()
    for k in (2, 1, 0):
        weights_copy(0, k).start()
    x_copy.start()
    lat_copy.wait()
    pl.semaphore_wait(barrier, n_time - 1)

    def cols(c):
        return slice(c * 128, (c + 1) * 128)

    def partial_sums(v):
        folded = v.reshape(v.shape[0] // 8, 8, 128)
        return jnp.sum(folded, axis=0), jnp.sum(folded * folded, axis=0)

    def latent_stats(n, carry):
        frame, row = n // ROWS, lax.rem(n, ROWS)
        new = []
        for c in range(4):
            s1, s2 = partial_sums(raw[frame, row, :, cols(c)].astype(F32))
            new += [carry[2 * c] + s1, carry[2 * c + 1] + s2]
        return tuple(new)

    sums = lax.fori_loop(0, 2 * ROWS, latent_stats, tuple(jnp.zeros((8, 128), F32) for _ in range(8)))
    for c in range(4):
        pstat[c] = sums[2 * c]
        pstat[4 + c] = sums[2 * c + 1]
    x_copy.wait()

    elem_count = float(n_time * 2 * ROWS * WIDTH * (CHANS // GROUPS))
    lane = lax.broadcasted_iota(jnp.int32, (8, 128), 1)
    sub16 = lax.broadcasted_iota(jnp.int32, (LANES, 128), 0)

    def exchange(layer, par):
        for n in range(8):
            srecv[par, me, n:n + 1, :] = jnp.sum(pstat[n], axis=0, keepdims=True)
        def stat_copy(d):
            return pltpu.make_async_remote_copy(
                src_ref=srecv.at[par, me], dst_ref=srecv.at[par, me],
                send_sem=stat_send.at[d], recv_sem=stat_recv.at[par, me],
                device_id={"cp": lax.rem(me + d, n_time)}, device_id_type=MESH)
        for d in range(1, n_time):
            stat_copy(d).start()

        @pl.when(layer == 0)
        def _():
            halo_copy(1, par).start()

        halo_copy(0, par).start()
        for d in range(1, n_time):
            src = lax.rem(me + n_time - d, n_time)
            pltpu.make_async_remote_copy(
                src_ref=srecv.at[par, src], dst_ref=srecv.at[par, src],
                send_sem=stat_send.at[d], recv_sem=stat_recv.at[par, src],
                device_id={"cp": src}, device_id_type=MESH).wait_recv()
        total = srecv[par, 0]
        for n in range(1, n_time):
            total = total + srecv[par, n]
        for s in (1, 2, 4, 8):
            total = total + jnp.where((lane & s) == 0, pltpu.roll(total, 128 - s, 1), pltpu.roll(total, s, 1))
        grp_mean = total[0:4] / elem_count
        grp_var = total[4:8] / elem_count - grp_mean * grp_mean
        scale = lax.rsqrt(grp_var + NORM_EPS) * gam_ref[layer]
        affine[0:4, :] = scale
        affine[4:8, :] = bet_ref[layer] - grp_mean * scale
        for d in range(1, n_time):
            stat_copy(d).wait_send()

    def norm_row(slot, row, dst):
        for c in range(4):
            v = raw[slot, row, :, cols(c)].astype(F32)
            u = (v * affine[c:c + 1, :] + affine[4 + c:5 + c, :]).astype(BF16).astype(F32)
            act = u * jax.nn.sigmoid(u)
            dst[row, LANES:LANES + WIDTH, cols(c)] = act.astype(BF16)
            before = pltpu.roll(act[WIDTH - LANES:], 1, 0)
            dst[row, 0:LANES, cols(c)] = jnp.where(sub16 == 0, 0.0, before).astype(BF16)
            after = pltpu.roll(act[:LANES], LANES - 1, 0)
            dst[row, LANES + WIDTH:, cols(c)] = jnp.where(sub16 == LANES - 1, 0.0, after).astype(BF16)

    def group(acc, act, w_slot, k, first, side=()):
        for s, di in enumerate((1, 0, 2)):
            lo, hi = max(0, 1 - di), min(ROWS, ROWS + 1 - di)
            lhs = jnp.concatenate(
                [act[lo + di - 1:hi + di - 1, LANES * dj:LANES * dj + WIDTH, :].reshape((hi - lo) * WIDTH, CHANS)
                 for dj in range(3)], axis=1)
            part = jnp.dot(lhs, wbuf[w_slot, k, di].reshape(3 * CHANS, CHANS), preferred_element_type=F32)
            part = part.reshape(hi - lo, WIDTH, CHANS)
            if first and s == 0:
                acc[...] = part
            else:
                acc[lo:hi] = acc[lo:hi] + part
            for step in side[s] if side else ():
                step()

    def epilogue(frame, row, acc, layer, odd, sums):
        for q in range(2):
            for half in range(2):
                c = 2 * q + half
                h = (acc[row, :, cols(c)] + bias_ref[layer, :, cols(c)]).astype(BF16).astype(F32)
                x_old = xbuf[frame, row, :, cols(c)].astype(F32)
                res = (jnp.where(odd, x_old, 0.0) + h).astype(BF16)
                wide = res.astype(F32)
                raw[frame, row, :, cols(c)] = res
                xbuf[frame, row, :, cols(c)] = jnp.where(odd, wide, x_old).astype(BF16)
                s1, s2 = partial_sums(wide)
                sums[c] = s1 if sums[c] is None else sums[c] + s1
                sums[4 + c] = s2 if sums[4 + c] is None else sums[4 + c] + s2

    def layer_body(layer, carry):
        par = lax.rem(layer, 2)
        odd = par == 1
        more = layer + 1 < N_LAYERS
        halo_0 = jnp.where(me == 0, 0, 2 + 2 * par)
        halo_1 = jnp.where(me == 0, 0, 3 + 2 * par)

        exchange(layer, par)
        for k in (2, 1, 0):
            weights_copy(layer, k).wait()

        @pl.when(more)
        def _():
            for k in (2, 1, 0):
                weights_copy(layer + 1, k).start()

        for row in range(ROWS):
            norm_row(1, row, a3)

        def spread(fn):
            return [[lambda r=r: fn(r) for r in (2 * n, 2 * n + 1)] for n in range(3)]

        group(acc1, a3, par, 2, True, spread(lambda r: norm_row(0, r, a2)))
        halo_copy(1, par).wait_recv()
        group(acc1, a2, par, 1, False, spread(lambda r: norm_row(halo_1, r, a1)))
        halo_copy(1, par).wait_send()
        group(acc1, a1, par, 0, False)

        def finish_frame_1():
            sums = [None] * 8
            for row in range(ROWS):
                epilogue(1, row, acc1, layer, odd, sums)
            for n in range(8):
                pstat[n] = sums[n]

            @pl.when(more)
            def _():
                halo_copy(1, 1 - par).start()

        group(acc0, a2, par, 2, True, [[finish_frame_1], [], []])
        halo_copy(0, par).wait()
        group(acc0, a1, par, 1, False, spread(lambda r: norm_row(halo_0, r, a0)))
        group(acc0, a0, par, 0, False)
        sums = [None] * 8
        for row in range(ROWS):
            epilogue(0, row, acc0, layer, odd, sums)
        for n in range(8):
            pstat[n] = pstat[n] + sums[n]
        return carry

    lax.fori_loop(0, N_LAYERS, layer_body, 0)

    out_copy = pltpu.make_async_copy(raw.at[pl.ds(0, 2)], out_ref, out_sem)
    out_copy.start()
    out_copy.wait()


def solution(mesh):
    n_time = mesh.shape["cp"]
    frame_spec = P(("dp", "cp"))

    def local_fn(latent, conv_kernels, conv_biases, gn_gammas, gn_betas):
        lat = latent.reshape(2, ROWS, LANES, RES, CHANS).transpose(0, 1, 3, 2, 4).reshape(2, ROWS, WIDTH, CHANS)
        act = pltpu.VMEM((ROWS, WIDTH + 2 * LANES, CHANS), BF16)
        any_spec = pl.BlockSpec(memory_space=pl.ANY)
        vmem_spec = pl.BlockSpec(memory_space=pltpu.VMEM)

        def run(*refs):
            return kernel(n_time, *refs)

        out = pl.pallas_call(
            run,
            out_shape=jax.ShapeDtypeStruct((2, ROWS, WIDTH, CHANS), BF16),
            in_specs=[any_spec, any_spec, vmem_spec, vmem_spec, vmem_spec],
            out_specs=any_spec,
            scratch_shapes=[
                pltpu.VMEM((6, ROWS, WIDTH, CHANS), BF16),
                pltpu.VMEM((2, ROWS, WIDTH, CHANS), BF16),
                pltpu.VMEM((ROWS, WIDTH, CHANS), F32),
                pltpu.VMEM((ROWS, WIDTH, CHANS), F32),
                act, act, act, act,
                pltpu.VMEM((2, 3, 3, 3, CHANS, CHANS), BF16),
                pltpu.VMEM((8, 128), F32),
                pltpu.VMEM((8, 8, 128), F32),
                pltpu.VMEM((2, n_time, 8, 128), F32),
                pltpu.SemaphoreType.DMA((2,)),
                pltpu.SemaphoreType.DMA((2, 3)),
                pltpu.SemaphoreType.DMA((n_time,)),
                pltpu.SemaphoreType.DMA((2, n_time)),
                pltpu.SemaphoreType.DMA((2,)),
                pltpu.SemaphoreType.DMA((2, 2)),
                pltpu.SemaphoreType.DMA,
            ],
            compiler_params=pltpu.CompilerParams(
                collective_id=0, has_side_effects=True, vmem_limit_bytes=60 * 1024 * 1024),
            name="resnet_blocks",
        )(lat, conv_kernels, conv_biases.reshape(N_LAYERS, 1, CHANS),
          gn_gammas.reshape(N_LAYERS, 4, 128), gn_betas.reshape(N_LAYERS, 4, 128))
        return out.reshape(2, ROWS, RES, LANES, CHANS).transpose(0, 1, 3, 2, 4).reshape(2, ROWS, WIDTH, CHANS)

    return jax.shard_map(local_fn, mesh=mesh, in_specs=(frame_spec, P(), P(), P(), P()), out_specs=frame_spec, check_vma=False)
```

time: 268 us -> 112 us (0.42)
  the two profiles are of different devices: /device:TPU:12 before, /device:TPU:0 now
where the time goes in v1:
time: 112 us
  Pallas kernels  100 us (89%)
  local copies, waits for them, and re-layouts  11.4 us (10%)
    pallas_call x1, Pallas kernels, local_fn(): pl.pallas_call(run, out_shape=jax.ShapeDtypeStruct((2, ROWS, WIDTH, CHANS...  100 us
    reshape x2, local copies, waits for them, and re-layouts, local_fn(): out.reshape(2, ROWS, RES, LANES, CHANS).transpose(0, 1, 3, 2, 4)  3.71 us
    unnamed x1, local copies, waits for them, and re-layouts  2.48 us

profile of v1, /device:TPU:0, one launch (start us, length us, event | category | flops | bytes accessed | tf_op | source)
XLA Modules:
  0.0 111.8 jit_solution(18069121384714864003)
XLA Ops:
  0.0 1.3 %reshape.23.refs_2_ = f32[4,1,512]{2,1,0:T(1,128)} reshape(f32[4,512]{1,0:T(4,128)} %param.7) | data formatting | bytes 16384 | tf_op jit(solution)/shard_map/reshape | solution.py:247
  1.3 1.3 %reshape.24.refs_3_ = f32[4,4,128]{2,1,0:T(4,128)} reshape(f32[4,512]{1,0:T(4,128)} %param.8) | data formatting | bytes 16384 | tf_op jit(solution)/shard_map/reshape | solution.py:248
  2.6 1.3 %reshape.25.refs_4_ = f32[4,4,128]{2,1,0:T(4,128)} reshape(f32[4,512]{1,0:T(4,128)} %param.9) | data formatting | bytes 16384 | tf_op jit(solution)/shard_map/reshape | solution.py:248
  3.9 2.5 %copy.8 = bf16[2,6,96,512]{3,0,2,1:T(2,128)(2,1)S(1)} copy(bf16[2,6,96,512]{3,2,1,0:T(8,128)(2,1)} %param.5) | data formatting | bytes 2359296 | tf_op args[0]
  6.4 1.3 %copy.9 = bf16[2,6,6,16,512]{4,3,2,1,0:T(8,128)(2,1)} copy(bf16[2,6,6,16,512]{4,0,2,3,1:T(2,128)(2,1)S(1)} %bitcast.9) | data formatting | bytes 2359296 | tf_op jit(solution)/shard_map/transpose | solution.py:213
  7.7 100.4 %resnet_blocks.1 = bf16[2,6,96,512]{3,2,1,0:T(8,128)(2,1)} custom-call(bf16[2,6,96,512]{3,2,1,0:T(8,128)(2,1)} %bitcast.10, bf16[4,3,3,3,512,512]{5,4,3,2,1,0:T(8,128)(2,1)} %refs_1_.1, f32[4,1,512]{2,1,0:T(1,128)} %reshape.23.refs_2_, f32[4,4,128]{2,1,0:T(4,128)} %reshape.24.refs_3_, f32[4,4,128]{2,1,0:T(4,128)} %reshape.25.refs_4_), custom_call_target="tpu_custom_call" | custom-call | tf_op jit(solution)/shard_map/resnet_blocks/pallas_call | solution.py:221
  108.1 2.5 %copy.10 = bf16[2,6,6,16,512]{4,0,2,3,1:T(2,128)(2,1)S(1)} copy(bf16[2,6,6,16,512]{4,3,2,1,0:T(8,128)(2,1)} %bitcast.11) | data formatting | bytes 2359296 | tf_op jit(solution)/shard_map/reshape | solution.py:249
  110.5 1.2 %copy.11 = bf16[2,6,96,512]{3,2,1,0:T(8,128)(2,1)} copy(bf16[2,6,96,512]{3,0,2,1:T(2,128)(2,1)S(1)} %bitcast.8) | data formatting | bytes 2359296 | tf_op jit(solution)/shard_map/reshape | solution.py:249

commit v2 on v1

--- a/solution.py
+++ b/solution.py
@@ -19,8 +19,8 @@
 
 
 def kernel(n_time, lat_ref, w_ref, bias_ref, gam_ref, bet_ref, out_ref,
-           raw, xbuf, acc0, acc1, a0, a1, a2, a3, wbuf, affine, pstat, srecv,
-           lat_sem, w_sem, stat_send, stat_recv, halo_send, halo_recv, out_sem):
+           raw, xbuf, acc0, acc1, a0, a1, a2, a3, wbuf, perm, params, affine, pstat, srecv,
+           lat_sem, w_sem, stat_send, stat_recv, halo_send, halo_recv):
     me = lax.axis_index("cp")
     nxt = lax.rem(me + 1, n_time)
     acts = (a0, a1, a2, a3)
@@ -39,14 +39,12 @@
             send_sem=halo_send.at[frame], recv_sem=halo_recv.at[par, frame],
             device_id={"cp": nxt}, device_id_type=MESH)
 
-    lat_copy = pltpu.make_async_copy(lat_ref, raw.at[pl.ds(0, 2)], lat_sem.at[0])
-    x_copy = pltpu.make_async_copy(lat_ref, xbuf, lat_sem.at[1])
+    lat_copy = pltpu.make_async_copy(lat_ref, out_ref, lat_sem)
     lat_copy.start()
-    for k in (2, 1, 0):
-        weights_copy(0, k).start()
-    x_copy.start()
-    lat_copy.wait()
-    pl.semaphore_wait(barrier, n_time - 1)
+    weights_copy(0, 2).start()
+    for n, ref in enumerate((bias_ref, gam_ref, bet_ref)):
+        for layer in range(N_LAYERS):
+            params[n, layer] = ref[layer:layer + 1, :]
 
     def cols(c):
         return slice(c * 128, (c + 1) * 128)
@@ -55,19 +53,27 @@
         folded = v.reshape(v.shape[0] // 8, 8, 128)
         return jnp.sum(folded, axis=0), jnp.sum(folded * folded, axis=0)
 
-    def latent_stats(n, carry):
+    def load_latent(n, carry):
         frame, row = n // ROWS, lax.rem(n, ROWS)
-        new = []
-        for c in range(4):
-            s1, s2 = partial_sums(raw[frame, row, :, cols(c)].astype(F32))
-            new += [carry[2 * c] + s1, carry[2 * c + 1] + s2]
+        new = list(carry)
+        for c in range(4):
+            perm[c] = out_ref[frame, row, :, cols(c)].astype(F32)
+            for r in range(RES):
+                v = perm[c, pl.ds(r, LANES, stride=RES), :]
+                here = (frame, row, slice(r * LANES, (r + 1) * LANES), cols(c))
+                raw[here] = v.astype(BF16)
+                xbuf[here] = v.astype(BF16)
+                s1, s2 = partial_sums(v)
+                new[2 * c] = new[2 * c] + s1
+                new[2 * c + 1] = new[2 * c + 1] + s2
         return tuple(new)
 
-    sums = lax.fori_loop(0, 2 * ROWS, latent_stats, tuple(jnp.zeros((8, 128), F32) for _ in range(8)))
+    lat_copy.wait()
+    sums = lax.fori_loop(0, 2 * ROWS, load_latent, tuple(jnp.zeros((8, 128), F32) for _ in range(8)))
     for c in range(4):
         pstat[c] = sums[2 * c]
         pstat[4 + c] = sums[2 * c + 1]
-    x_copy.wait()
+    pl.semaphore_wait(barrier, n_time - 1)
 
     elem_count = float(n_time * 2 * ROWS * WIDTH * (CHANS // GROUPS))
     lane = lax.broadcasted_iota(jnp.int32, (8, 128), 1)
@@ -86,15 +92,21 @@
 
         @pl.when(layer == 0)
         def _():
-            halo_copy(1, par).start()
-
-        halo_copy(0, par).start()
+            weights_copy(0, 1).start()
+            weights_copy(0, 0).start()
+
         for d in range(1, n_time):
             src = lax.rem(me + n_time - d, n_time)
             pltpu.make_async_remote_copy(
                 src_ref=srecv.at[par, src], dst_ref=srecv.at[par, src],
                 send_sem=stat_send.at[d], recv_sem=stat_recv.at[par, src],
                 device_id={"cp": src}, device_id_type=MESH).wait_recv()
+
+        @pl.when(layer == 0)
+        def _():
+            halo_copy(1, par).start()
+
+        halo_copy(0, par).start()
         total = srecv[par, 0]
         for n in range(1, n_time):
             total = total + srecv[par, n]
@@ -102,9 +114,11 @@
             total = total + jnp.where((lane & s) == 0, pltpu.roll(total, 128 - s, 1), pltpu.roll(total, s, 1))
         grp_mean = total[0:4] / elem_count
         grp_var = total[4:8] / elem_count - grp_mean * grp_mean
-        scale = lax.rsqrt(grp_var + NORM_EPS) * gam_ref[layer]
-        affine[0:4, :] = scale
-        affine[4:8, :] = bet_ref[layer] - grp_mean * scale
+        inv = lax.rsqrt(grp_var + NORM_EPS)
+        for c in range(4):
+            scale = inv[c:c + 1] * params[1, layer, :, cols(c)]
+            affine[c:c + 1, :] = scale
+            affine[4 + c:5 + c, :] = params[2, layer, :, cols(c)] - grp_mean[c:c + 1] * scale
         for d in range(1, n_time):
             stat_copy(d).wait_send()
 
@@ -138,7 +152,7 @@
         for q in range(2):
             for half in range(2):
                 c = 2 * q + half
-                h = (acc[row, :, cols(c)] + bias_ref[layer, :, cols(c)]).astype(BF16).astype(F32)
+                h = (acc[row, :, cols(c)] + params[0, layer, :, cols(c)]).astype(BF16).astype(F32)
                 x_old = xbuf[frame, row, :, cols(c)].astype(F32)
                 res = (jnp.where(odd, x_old, 0.0) + h).astype(BF16)
                 wide = res.astype(F32)
@@ -200,9 +214,15 @@
 
     lax.fori_loop(0, N_LAYERS, layer_body, 0)
 
-    out_copy = pltpu.make_async_copy(raw.at[pl.ds(0, 2)], out_ref, out_sem)
-    out_copy.start()
-    out_copy.wait()
+    def store_row(n, carry):
+        frame, row = n // ROWS, lax.rem(n, ROWS)
+        for c in range(4):
+            for r in range(RES):
+                perm[c, pl.ds(r, LANES, stride=RES), :] = raw[frame, row, r * LANES:(r + 1) * LANES, cols(c)].astype(F32)
+            out_ref[frame, row, :, cols(c)] = perm[c].astype(BF16)
+        return carry
+
+    lax.fori_loop(0, 2 * ROWS, store_row, 0)
 
 
 def solution(mesh):
@@ -210,7 +230,6 @@
     frame_spec = P(("dp", "cp"))
 
     def local_fn(latent, conv_kernels, conv_biases, gn_gammas, gn_betas):
-        lat = latent.reshape(2, ROWS, LANES, RES, CHANS).transpose(0, 1, 3, 2, 4).reshape(2, ROWS, WIDTH, CHANS)
         act = pltpu.VMEM((ROWS, WIDTH + 2 * LANES, CHANS), BF16)
         any_spec = pl.BlockSpec(memory_space=pl.ANY)
         vmem_spec = pl.BlockSpec(memory_space=pltpu.VMEM)
@@ -218,11 +237,11 @@
         def run(*refs):
             return kernel(n_time, *refs)
 
-        out = pl.pallas_call(
+        return pl.pallas_call(
             run,
             out_shape=jax.ShapeDtypeStruct((2, ROWS, WIDTH, CHANS), BF16),
             in_specs=[any_spec, any_spec, vmem_spec, vmem_spec, vmem_spec],
-            out_specs=any_spec,
+            out_specs=vmem_spec,
             scratch_shapes=[
                 pltpu.VMEM((6, ROWS, WIDTH, CHANS), BF16),
                 pltpu.VMEM((2, ROWS, WIDTH, CHANS), BF16),
@@ -230,22 +249,21 @@
                 pltpu.VMEM((ROWS, WIDTH, CHANS), F32),
                 act, act, act, act,
                 pltpu.VMEM((2, 3, 3, 3, CHANS, CHANS), BF16),
+                pltpu.VMEM((4, WIDTH, 128), F32),
+                pltpu.VMEM((3, N_LAYERS, 1, CHANS), F32),
                 pltpu.VMEM((8, 128), F32),
                 pltpu.VMEM((8, 8, 128), F32),
                 pltpu.VMEM((2, n_time, 8, 128), F32),
-                pltpu.SemaphoreType.DMA((2,)),
+                pltpu.SemaphoreType.DMA,
                 pltpu.SemaphoreType.DMA((2, 3)),
                 pltpu.SemaphoreType.DMA((n_time,)),
                 pltpu.SemaphoreType.DMA((2, n_time)),
                 pltpu.SemaphoreType.DMA((2,)),
                 pltpu.SemaphoreType.DMA((2, 2)),
-                pltpu.SemaphoreType.DMA,
             ],
             compiler_params=pltpu.CompilerParams(
                 collective_id=0, has_side_effects=True, vmem_limit_bytes=60 * 1024 * 1024),
             name="resnet_blocks",
-        )(lat, conv_kernels, conv_biases.reshape(N_LAYERS, 1, CHANS),
-          gn_gammas.reshape(N_LAYERS, 4, 128), gn_betas.reshape(N_LAYERS, 4, 128))
-        return out.reshape(2, ROWS, RES, LANES, CHANS).transpose(0, 1, 3, 2, 4).reshape(2, ROWS, WIDTH, CHANS)
+        )(latent, conv_kernels, conv_biases, gn_gammas, gn_betas)
 
     return jax.shard_map(local_fn, mesh=mesh, in_specs=(frame_spec, P(), P(), P(), P()), out_specs=frame_spec, check_vma=False)

time: 112 us -> 92.2 us (0.82)
  Pallas kernels: 100 us -> 89.6 us
  local copies, waits for them, and re-layouts: 11.4 us -> 2.36 us
    pallas_call x1, Pallas kernels: 100 us -> 89.6 us  [local_fn(): pl.pallas_call(run, out_shape=jax.ShapeDtypeStruct((2, ROWS, WIDTH, CHANS...]
    reshape x5 -> x0, local copies, waits for them, and re-layouts: 7.61 us -> none  [the longest x2 3.71 us: local_fn(): out.reshape(2, ROWS, RES, LANES, CHANS).transpose(0, 1, 3, 2, 4)]
    transpose x1 -> x0, local copies, waits for them, and re-layouts: 1.29 us -> none  [local_fn(): latent.reshape(2, ROWS, LANES, RES, CHANS).transpose(0, 1, 3, 2, 4)]
where the time goes in v2:
time: 92.2 us; the launch traced here: 92 us
  Pallas kernels  89.6 us (97%)
  local copies, waits for them, and re-layouts  2.36 us (3%)
    pallas_call x1, Pallas kernels, local_fn(): pl.pallas_call(run, out_shape=jax.ShapeDtypeStruct((2, ROWS, WIDTH, CHANS...  89.6 us
    unnamed x1, local copies, waits for them, and re-layouts  2.36 us

profile of v2, /device:TPU:0, one launch (start us, length us, event | category | flops | bytes accessed | tf_op | source)
XLA Modules:
  0.0 92.0 jit_solution(18053683584935260571)
XLA Ops:
  0.0 89.6 %resnet_blocks.1 = bf16[2,6,96,512]{3,2,1,0:T(8,128)(2,1)} custom-call(bf16[2,6,96,512]{3,2,1,0:T(8,128)(2,1)} %refs_0_.1, bf16[4,3,3,3,512,512]{5,4,3,2,1,0:T(8,128)(2,1)} %refs_1_.1, f32[4,512]{1,0:T(4,128)} %refs_2_.1, f32[4,512]{1,0:T(4,128)} %refs_3_.1, f32[4,512]{1,0:T(4,128)} %refs_4_.1), custom_call_target="tpu_custom_call" | custom-call | tf_op jit(solution)/shard_map/resnet_blocks/pallas_call | solution.py:240
  89.6 2.4 %copy.7 = bf16[2,6,96,512]{3,2,1,0:T(8,128)(2,1)} copy(bf16[2,6,96,512]{3,2,1,0:T(8,128)(2,1)} %resnet_blocks.1) | data formatting | bytes 2359296

commit v3 on v2

--- a/solution.py
+++ b/solution.py
@@ -53,47 +53,48 @@
         folded = v.reshape(v.shape[0] // 8, 8, 128)
         return jnp.sum(folded, axis=0), jnp.sum(folded * folded, axis=0)
 
-    def load_latent(n, carry):
+    def latent_sums(n, carry):
         frame, row = n // ROWS, lax.rem(n, ROWS)
-        new = list(carry)
+        new = []
+        for c in range(4):
+            s1, s2 = partial_sums(out_ref[frame, row, :, cols(c)].astype(F32))
+            new += [carry[2 * c] + s1, carry[2 * c + 1] + s2]
+        return tuple(new)
+
+    def permute_latent(n, carry):
+        frame, row = n // ROWS, lax.rem(n, ROWS)
         for c in range(4):
             perm[c] = out_ref[frame, row, :, cols(c)].astype(F32)
             for r in range(RES):
-                v = perm[c, pl.ds(r, LANES, stride=RES), :]
+                v = perm[c, pl.ds(r, LANES, stride=RES), :].astype(BF16)
                 here = (frame, row, slice(r * LANES, (r + 1) * LANES), cols(c))
-                raw[here] = v.astype(BF16)
-                xbuf[here] = v.astype(BF16)
-                s1, s2 = partial_sums(v)
-                new[2 * c] = new[2 * c] + s1
-                new[2 * c + 1] = new[2 * c + 1] + s2
-        return tuple(new)
+                raw[here] = v
+                xbuf[here] = v
+        return carry
 
     lat_copy.wait()
-    sums = lax.fori_loop(0, 2 * ROWS, load_latent, tuple(jnp.zeros((8, 128), F32) for _ in range(8)))
+    sums = lax.fori_loop(0, 2 * ROWS, latent_sums, tuple(jnp.zeros((8, 128), F32) for _ in range(8)))
     for c in range(4):
         pstat[c] = sums[2 * c]
         pstat[4 + c] = sums[2 * c + 1]
-    pl.semaphore_wait(barrier, n_time - 1)
 
     elem_count = float(n_time * 2 * ROWS * WIDTH * (CHANS // GROUPS))
     lane = lax.broadcasted_iota(jnp.int32, (8, 128), 1)
     sub16 = lax.broadcasted_iota(jnp.int32, (LANES, 128), 0)
 
-    def exchange(layer, par):
+    def stat_copy(par, d):
+        return pltpu.make_async_remote_copy(
+            src_ref=srecv.at[par, me], dst_ref=srecv.at[par, me],
+            send_sem=stat_send.at[d], recv_sem=stat_recv.at[par, me],
+            device_id={"cp": lax.rem(me + d, n_time)}, device_id_type=MESH)
+
+    def sums_out(par):
         for n in range(8):
             srecv[par, me, n:n + 1, :] = jnp.sum(pstat[n], axis=0, keepdims=True)
-        def stat_copy(d):
-            return pltpu.make_async_remote_copy(
-                src_ref=srecv.at[par, me], dst_ref=srecv.at[par, me],
-                send_sem=stat_send.at[d], recv_sem=stat_recv.at[par, me],
-                device_id={"cp": lax.rem(me + d, n_time)}, device_id_type=MESH)
         for d in range(1, n_time):
-            stat_copy(d).start()
-
-        @pl.when(layer == 0)
-        def _():
-            weights_copy(0, 1).start()
-            weights_copy(0, 0).start()
+            stat_copy(par, d).start()
+
+    def sums_in(layer, par):
 
         for d in range(1, n_time):
             src = lax.rem(me + n_time - d, n_time)
@@ -120,7 +121,13 @@
             affine[c:c + 1, :] = scale
             affine[4 + c:5 + c, :] = params[2, layer, :, cols(c)] - grp_mean[c:c + 1] * scale
         for d in range(1, n_time):
-            stat_copy(d).wait_send()
+            stat_copy(par, d).wait_send()
+
+    pl.semaphore_wait(barrier, n_time - 1)
+    sums_out(0)
+    weights_copy(0, 1).start()
+    weights_copy(0, 0).start()
+    lax.fori_loop(0, 2 * ROWS, permute_latent, 0)
 
     def norm_row(slot, row, dst):
         for c in range(4):
@@ -133,19 +140,22 @@
             after = pltpu.roll(act[:LANES], LANES - 1, 0)
             dst[row, LANES + WIDTH:, cols(c)] = jnp.where(sub16 == LANES - 1, 0.0, after).astype(BF16)
 
-    def group(acc, act, w_slot, k, first, side=()):
-        for s, di in enumerate((1, 0, 2)):
-            lo, hi = max(0, 1 - di), min(ROWS, ROWS + 1 - di)
+    def group(acc, act, w_slot, k, first, side=None, parts=1):
+        side = side or {}
+        height = ROWS // parts
+        steps = [(part, di) for part in range(parts) for di in (1, 0, 2)]
+        for n, (part, di) in enumerate(steps):
+            lo, hi = max(height * part, 1 - di), min(height * (part + 1), ROWS + 1 - di)
             lhs = jnp.concatenate(
                 [act[lo + di - 1:hi + di - 1, LANES * dj:LANES * dj + WIDTH, :].reshape((hi - lo) * WIDTH, CHANS)
                  for dj in range(3)], axis=1)
-            part = jnp.dot(lhs, wbuf[w_slot, k, di].reshape(3 * CHANS, CHANS), preferred_element_type=F32)
-            part = part.reshape(hi - lo, WIDTH, CHANS)
-            if first and s == 0:
-                acc[...] = part
+            prod = jnp.dot(lhs, wbuf[w_slot, k, di].reshape(3 * CHANS, CHANS), preferred_element_type=F32)
+            prod = prod.reshape(hi - lo, WIDTH, CHANS)
+            if first and di == 1:
+                acc[lo:hi] = prod
             else:
-                acc[lo:hi] = acc[lo:hi] + part
-            for step in side[s] if side else ():
+                acc[lo:hi] = acc[lo:hi] + prod
+            for step in side.get(n, ()):
                 step()
 
     def epilogue(frame, row, acc, layer, odd, sums):
@@ -166,10 +176,11 @@
         par = lax.rem(layer, 2)
         odd = par == 1
         more = layer + 1 < N_LAYERS
+        later = layer > 0
         halo_0 = jnp.where(me == 0, 0, 2 + 2 * par)
         halo_1 = jnp.where(me == 0, 0, 3 + 2 * par)
 
-        exchange(layer, par)
+        sums_in(layer, par)
         for k in (2, 1, 0):
             weights_copy(layer, k).wait()
 
@@ -178,21 +189,40 @@
             for k in (2, 1, 0):
                 weights_copy(layer + 1, k).start()
 
-        for row in range(ROWS):
+        for row in range(4):
             norm_row(1, row, a3)
 
-        def spread(fn):
-            return [[lambda r=r: fn(r) for r in (2 * n, 2 * n + 1)] for n in range(3)]
-
-        group(acc1, a3, par, 2, True, spread(lambda r: norm_row(0, r, a2)))
-        halo_copy(1, par).wait_recv()
-        group(acc1, a2, par, 1, False, spread(lambda r: norm_row(halo_1, r, a1)))
+        def normed(slot, dst, plan):
+            return {n: [lambda r=r: norm_row(slot, r, dst) for r in rows] for n, rows in plan.items()}
+
+        def finished(frame, acc, sums, plan):
+            return {n: [lambda r=r: epilogue(frame, r, acc, layer, odd, sums) for r in rows] for n, rows in plan.items()}
+
+        side = normed(0, a2, {1: (0,), 2: (1,), 3: (2,), 4: (3, 4), 5: (5,)})
+        side[0] = [lambda r=r: norm_row(1, r, a3) for r in (4, 5)]
+        group(acc1, a3, par, 2, True, side, 2)
+        @pl.when(later)
+        def _():
+            halo_copy(1, par).wait_recv()
+
+        group(acc1, a2, par, 1, False, normed(jnp.where(later, halo_1, 0), a1, {0: (0, 1), 1: (2, 3), 2: (4, 5)}))
+
+        @pl.when(layer == 0)
+        def _():
+            halo_copy(1, par).wait_recv()
+
+            def row_step(row, carry):
+                norm_row(halo_1, row, a1)
+                return carry
+
+            lax.fori_loop(0, ROWS, row_step, 0)
+
         halo_copy(1, par).wait_send()
-        group(acc1, a1, par, 0, False)
+        sums = [None] * 8
+        group(acc1, a1, par, 0, False, finished(1, acc1, sums, {3: (0,), 4: (1,), 5: (2,)}), 2)
 
         def finish_frame_1():
-            sums = [None] * 8
-            for row in range(ROWS):
+            for row in (3, 4, 5):
                 epilogue(1, row, acc1, layer, odd, sums)
             for n in range(8):
                 pstat[n] = sums[n]
@@ -201,28 +231,46 @@
             def _():
                 halo_copy(1, 1 - par).start()
 
-        group(acc0, a2, par, 2, True, [[finish_frame_1], [], []])
+        group(acc0, a2, par, 2, True, {0: [finish_frame_1]})
         halo_copy(0, par).wait()
-        group(acc0, a1, par, 1, False, spread(lambda r: norm_row(halo_0, r, a0)))
-        group(acc0, a0, par, 0, False)
-        sums = [None] * 8
-        for row in range(ROWS):
-            epilogue(0, row, acc0, layer, odd, sums)
+        group(acc0, a1, par, 1, False, normed(halo_0, a0, {0: (0, 1), 1: (2, 3), 2: (4, 5)}))
+        sums_0 = [None] * 8
+        group(acc0, a0, par, 0, False, finished(0, acc0, sums_0, {3: (0,), 4: (1,), 5: (2,)}), 2)
+        for row in (3, 4, 5):
+            epilogue(0, row, acc0, layer, odd, sums_0)
         for n in range(8):
-            pstat[n] = pstat[n] + sums[n]
+            pstat[n] = pstat[n] + sums_0[n]
+
+        @pl.when(more)
+        def _():
+            sums_out(1 - par)
+
         return carry
 
     lax.fori_loop(0, N_LAYERS, layer_body, 0)
+
+    out_ref[...] = raw[0:2]
+
+
+def unpermute(in_ref, out_ref, perm, rows, sems):
+    def cols(c):
+        return slice(c * 128, (c + 1) * 128)
+
+    def row_copy(n):
+        return pltpu.make_async_copy(rows.at[n], out_ref.at[n // ROWS, n % ROWS], sems.at[n])
 
     def store_row(n, carry):
         frame, row = n // ROWS, lax.rem(n, ROWS)
         for c in range(4):
             for r in range(RES):
-                perm[c, pl.ds(r, LANES, stride=RES), :] = raw[frame, row, r * LANES:(r + 1) * LANES, cols(c)].astype(F32)
-            out_ref[frame, row, :, cols(c)] = perm[c].astype(BF16)
+                perm[c, pl.ds(r, LANES, stride=RES), :] = in_ref[frame, row, r * LANES:(r + 1) * LANES, cols(c)].astype(F32)
+            rows[n, :, cols(c)] = perm[c].astype(BF16)
+        row_copy(n).start()
         return carry
 
     lax.fori_loop(0, 2 * ROWS, store_row, 0)
+    for n in range(2 * ROWS):
+        row_copy(n).wait()
 
 
 def solution(mesh):
@@ -237,7 +285,7 @@
         def run(*refs):
             return kernel(n_time, *refs)
 
-        return pl.pallas_call(
+        permuted = pl.pallas_call(
             run,
             out_shape=jax.ShapeDtypeStruct((2, ROWS, WIDTH, CHANS), BF16),
             in_specs=[any_spec, any_spec, vmem_spec, vmem_spec, vmem_spec],
@@ -265,5 +313,17 @@
                 collective_id=0, has_side_effects=True, vmem_limit_bytes=60 * 1024 * 1024),
             name="resnet_blocks",
         )(latent, conv_kernels, conv_biases, gn_gammas, gn_betas)
+        return pl.pallas_call(
+            unpermute,
+            out_shape=jax.ShapeDtypeStruct((2, ROWS, WIDTH, CHANS), BF16),
+            in_specs=[vmem_spec],
+            out_specs=any_spec,
+            scratch_shapes=[
+                pltpu.VMEM((4, WIDTH, 128), F32),
+                pltpu.VMEM((2 * ROWS, WIDTH, CHANS), BF16),
+                pltpu.SemaphoreType.DMA((2 * ROWS,)),
+            ],
+            name="unpermute",
+        )(permuted)
 
     return jax.shard_map(local_fn, mesh=mesh, in_specs=(frame_spec, P(), P(), P(), P()), out_specs=frame_spec, check_vma=False)

time: 92.2 us -> 90.2 us (0.978)
  local copies, waits for them, and re-layouts: 2.36 us -> 0 us
    pallas_call x0 -> x1, Pallas kernels: none -> 2.49 us  [local_fn(): pl.pallas_call(unpermute, out_shape=jax.ShapeDtypeStruct((2, ROWS, WIDTH,...]
    unnamed x1 -> x0, local copies, waits for them, and re-layouts: 2.36 us -> none
    pallas_call x1, Pallas kernels: 89.6 us -> 87.5 us  [local_fn(): pl.pallas_call(run, out_shape=jax.ShapeDtypeStruct((2, ROWS, WIDTH, CHANS...]
where the time goes in v3:
time: 90.2 us; the launch traced here: 90 us
  Pallas kernels  90 us (100%)
    pallas_call x1, Pallas kernels, local_fn(): pl.pallas_call(run, out_shape=jax.ShapeDtypeStruct((2, ROWS, WIDTH, CHANS...  87.5 us
    pallas_call x1, Pallas kernels, local_fn(): pl.pallas_call(unpermute, out_shape=jax.ShapeDtypeStruct((2, ROWS, WIDTH,...  2.49 us

profile of v3, /device:TPU:0, one launch (start us, length us, event | category | flops | bytes accessed | tf_op | source)
XLA Modules:
  0.0 90.0 jit_solution(4482057266415008356)
XLA Ops:
  0.0 87.5 %resnet_blocks.1.in_ref = bf16[2,6,96,512]{3,2,1,0:T(8,128)(2,1)} custom-call(bf16[2,6,96,512]{3,2,1,0:T(8,128)(2,1)} %refs_0_.1, bf16[4,3,3,3,512,512]{5,4,3,2,1,0:T(8,128)(2,1)} %refs_1_.1, f32[4,512]{1,0:T(4,128)} %refs_2_.1, f32[4,512]{1,0:T(4,128)} %refs_3_.1, f32[4,512]{1,0:T(4,128)} %refs_4_.1), custom_call_target="tpu_custom_call" | custom-call | tf_op jit(solution)/shard_map/resnet_blocks/pallas_call | solution.py:288
  87.5 2.5 %unpermute.1 = bf16[2,6,96,512]{3,2,1,0:T(8,128)(2,1)} custom-call(bf16[2,6,96,512]{3,2,1,0:T(8,128)(2,1)} %resnet_blocks.1.in_ref), custom_call_target="tpu_custom_call" | custom-call | tf_op jit(solution)/shard_map/unpermute/pallas_call | solution.py:316

commit v4 on v3

--- a/solution.py
+++ b/solution.py
@@ -107,7 +107,6 @@
         def _():
             halo_copy(1, par).start()
 
-        halo_copy(0, par).start()
         total = srecv[par, 0]
         for n in range(1, n_time):
             total = total + srecv[par, n]
@@ -191,6 +190,7 @@
 
         for row in range(4):
             norm_row(1, row, a3)
+        halo_copy(0, par).start()
 
         def normed(slot, dst, plan):
             return {n: [lambda r=r: norm_row(slot, r, dst) for r in rows] for n, rows in plan.items()}

time: 90.2 us -> 90 us (level)
  no operation moved by 1% of the time
where the time goes in v4:
time: 90 us; the launch traced here: 89.8 us
  Pallas kernels  89.7 us (100%)
    pallas_call x1, Pallas kernels, local_fn(): pl.pallas_call(run, out_shape=jax.ShapeDtypeStruct((2, ROWS, WIDTH, CHANS...  87.3 us
    pallas_call x1, Pallas kernels, local_fn(): pl.pallas_call(unpermute, out_shape=jax.ShapeDtypeStruct((2, ROWS, WIDTH,...  2.49 us

profile of v4, /device:TPU:0, one launch (start us, length us, event | category | flops | bytes accessed | tf_op | source)
XLA Modules:
  0.0 89.8 jit_solution(9495446742867064983)
XLA Ops:
  0.0 87.3 %resnet_blocks.1.in_ref = bf16[2,6,96,512]{3,2,1,0:T(8,128)(2,1)} custom-call(bf16[2,6,96,512]{3,2,1,0:T(8,128)(2,1)} %refs_0_.1, bf16[4,3,3,3,512,512]{5,4,3,2,1,0:T(8,128)(2,1)} %refs_1_.1, f32[4,512]{1,0:T(4,128)} %refs_2_.1, f32[4,512]{1,0:T(4,128)} %refs_3_.1, f32[4,512]{1,0:T(4,128)} %refs_4_.1), custom_call_target="tpu_custom_call" | custom-call | tf_op jit(solution)/shard_map/resnet_blocks/pallas_call | solution.py:288
  87.3 2.5 %unpermute.1 = bf16[2,6,96,512]{3,2,1,0:T(8,128)(2,1)} custom-call(bf16[2,6,96,512]{3,2,1,0:T(8,128)(2,1)} %resnet_blocks.1.in_ref), custom_call_target="tpu_custom_call" | custom-call | tf_op jit(solution)/shard_map/unpermute/pallas_call | solution.py:316
